TPU v7x, 32 devices: a whole 2x2x4 slice. The times are simulated.
32 devices in a mesh: row: 4 (over y, x), col: 8 (over z, core).
Axes of the slice: x: 2, y: 2, z: 4, core: 2. Of those that a mesh axis runs over, the one named last changes fastest.
Arguments:
- psi: bfloat16 [8192, 8192], P(('row', 'col')), may hold values from -0.125 to 0.125
- hpsi: bfloat16 [8192, 128], P(('row', 'col')), may hold values from -0.796875 to 0.796875
- slab_counts: int32 [32], P(('row', 'col')), may hold values from 1 to 256, 6144 in all
- matrix: float32 [4, 2048, 8, 1024], P('row', None, 'col'), as said below
Outputs:
- reduced: float32 [4, 2048, 8, 1024], P('row', None, 'col')
Inputs may be any that keep to these rules, and one draw needn't show every extreme that they name: Slab k's live plane waves are its first slab_counts[k] slots; the rest are padding; the counts sum to 3 * 256 * 32 // 4. The stored matrix is symmetric.
All inputs are finite; a program needn't handle non-finite values.
Results may differ from a plain program's by a relative error of at most 0.0003.
Values sent between devices are 32-bit elements; how exact they have to be, the bound alone decides.
No kernel may reach another device: no remote copies, remote signals or barrier semaphores. Data moves between devices by JAX's collectives and lax.ppermute only.
A program may use at most 64 MiB of HBM per device.

v0:
```python
import jax
import jax.numpy as jnp
from jax import lax
from jax.sharding import PartitionSpec as P

TILE = 16
HIGH = lax.Precision.HIGHEST


def lower_solve(factor, rhs):
    return lax.linalg.triangular_solve(factor, rhs, left_side=True, lower=True)


def invert_shifted(shifted):
    normal = jnp.dot(shifted.T, shifted, precision=HIGH)
    factor = jnp.linalg.cholesky(normal)
    first = lower_solve(factor, shifted.T)
    return lax.linalg.triangular_solve(factor, first, left_side=True, lower=True, transpose_a=True)


def per_device(psi, hpsi, slab_counts, matrix):
    prow_id = lax.axis_index("row")
    pcol_id = lax.axis_index("col")
    n_row = lax.axis_size("row")
    n_col = lax.axis_size("col")
    slots = psi.shape[0]
    panel = hpsi.shape[1]
    local_rows = matrix.shape[1]
    local_cols = matrix.shape[3]
    tiles_r = local_rows // TILE
    tiles_c = local_cols // TILE
    valid = jnp.arange(slots, dtype=jnp.int32) < slab_counts[0]
    hcols = jnp.where(valid[:, None], hpsi, jnp.zeros_like(hpsi))
    local_r = jnp.arange(local_rows, dtype=jnp.int32)
    local_c = jnp.arange(local_cols, dtype=jnp.int32)
    row_global = (local_r // TILE * n_row + prow_id) * TILE + local_r % TILE
    col_global = (local_c // TILE * n_col + pcol_id) * TILE + local_c % TILE
    partial_value = lax.dot_general(
        psi, hcols, (((0,), (0,)), ((), ())), preferred_element_type=jnp.float32
    )
    whole = lax.psum(partial_value, ("row", "col"))
    prow = lax.dynamic_index_in_dim(
        whole.reshape(tiles_r, n_row, TILE, panel), prow_id, 1, keepdims=False
    ).reshape(local_rows, panel)
    scols = lax.dynamic_index_in_dim(
        whole.reshape(tiles_c, n_col, TILE, panel), pcol_id, 1, keepdims=False
    ).reshape(local_cols, panel)
    span = jnp.arange(panel, dtype=jnp.int32)
    lower_r = jnp.where((row_global >= panel)[:, None], prow, jnp.zeros_like(prow))
    lower_c = jnp.where((col_global >= panel)[:, None], scols, jnp.zeros_like(scols))
    top_select = (row_global[None, :] == panel + span[:, None]).astype(jnp.float32)
    gram_part = jnp.dot(lower_r.T, lower_r, precision=HIGH)
    top_part = jnp.dot(top_select, prow, precision=HIGH)
    gram, top_rows = lax.psum((gram_part, top_part), "row")
    factor = jnp.linalg.cholesky(gram)
    basis_r = lower_solve(factor, lower_r.T).T
    basis_c = lower_solve(factor, lower_c.T).T
    top = lower_solve(factor, top_rows.T).T
    inverse = invert_shifted(jnp.eye(panel, dtype=jnp.float32) - top)
    embed_r = (row_global[:, None] == panel + span[None, :]).astype(jnp.float32)
    embed_c = (col_global[:, None] == panel + span[None, :]).astype(jnp.float32)
    reflect_r = basis_r - embed_r
    reflect_c = basis_c - embed_c
    stored = matrix[0, :, 0, :]
    col_select = (col_global[None, :] == span[:, None]).astype(jnp.float32)
    row_select = (row_global[None, :] == span[:, None]).astype(jnp.float32)
    left = jnp.dot(prow, col_select, precision=HIGH)
    upper = lax.dot_general(row_select, scols, (((0,), (1,)), ((), ())), precision=HIGH)
    inside_r = (row_global < panel)[:, None]
    inside_c = (col_global < panel)[None, :]
    refreshed = jnp.where(
        inside_r & inside_c,
        0.5 * (left + upper),
        jnp.where(inside_c, left, jnp.where(inside_r, upper, stored)),
    )
    zpart = jnp.dot(refreshed, reflect_c, precision=HIGH)
    zrows = lax.psum(zpart, "col")
    upart = lax.dot_general(refreshed, reflect_r, (((0,), (0,)), ((), ())), precision=HIGH)
    ucols = lax.psum(upart, "row")
    wmat = lax.psum(jnp.dot(reflect_r.T, zrows, precision=HIGH), "row")
    core = jnp.dot(jnp.dot(inverse, wmat, precision=HIGH), inverse.T, precision=HIGH)
    first = jnp.dot(reflect_r, jnp.dot(inverse, ucols.T, precision=HIGH), precision=HIGH)
    second = jnp.dot(
        jnp.dot(zrows, inverse.T, precision=HIGH) - jnp.dot(reflect_r, core, precision=HIGH),
        reflect_c.T,
        precision=HIGH,
    )
    return (refreshed - first - second)[None, :, None, :]


def solution(mesh):
    in_specs = (
        P(("row", "col"), None),
        P(("row", "col"), None),
        P(("row", "col")),
        P("row", None, "col", None),
    )
    out_specs = P("row", None, "col", None)
    return jax.shard_map(
        per_device, mesh=mesh, in_specs=in_specs, out_specs=out_specs, check_vma=False
    )
```

profile of v0, /device:TPU:0, one launch (start us, length us, event | category | flops | bytes accessed | tf_op | source)
XLA Modules:
  0.0 421.6 jit_solution(14257435263756658271)
XLA Ops:
  7.2 5.1 %convolution_bitcast_fusion = f32[8192,128]{0,1:T(8,128)} fusion(bf16[256,8192]{1,0:T(8,128)(2,1)} %param.7, bf16[256,128]{1,0:T(8,128)(2,1)} %param.8, pred[256]{0:T(512)(128)(4,1)S(1)} %iota_compare_fusion.9), kind=kOutput, calls=%fused_computation | convolution fusion | flops 536903680 | bytes 8454400 | tf_op jit(solution)/shard_map/dot_general | solution.py:38
  12.3 0.0 all-reduce.6.cloned.1.call-update
  12.3 0.0 all-reduce.8.cloned.1.call-start
  12.5 0.1 fusion.18
  12.6 145.3 %all-reduce.6.cloned.1.call-done = f32[8192,128]{0,1:T(8,128)} async-done(((f32[8192,128]{0,1:T(8,128)}), f32[8192,128]{0,1:T(8,128)}) %all-reduce.6.cloned.1.call-update) | async-done | bytes 4194320 | tf_op jit(solution)/shard_map/psum | solution.py:41
  157.9 5.6 %copy.11 = f32[8192,128]{1,0:T(8,128)} copy(f32[8192,128]{0,1:T(8,128)} %all-reduce.6.cloned.1.call-done) | data formatting | bytes 8388608 | tf_op jit(solution)/shard_map/psum | solution.py:41
  163.4 1.6 broadcast_select_fusion
  165.0 2.4 convolution_bitcast_fusion.1
  167.5 0.0 all-reduce.8.cloned.1.call-update
  167.5 0.0 all-reduce.10.cloned.1.call-start
  167.5 3.6 fusion.10
  171.1 1.3 broadcast_select_fusion.1
  172.4 11.0 %fusion.1 = f32[2048,1024]{1,0:T(8,128)} fusion(f32[2048,1024]{1,0:T(8,128)S(1)} %fusion.10, f32[1,2048,1,1024]{3,2,1,0:T(1,128)} %param.10, pred[1024]{0:T(1024)(128)(4,1)S(1)} %broadcast_compare_fusion.1, pred[2048]{0:T(1024)(128)(4,1)S(1)} %broadcast_compare_fusion, f32[1024,128]{1,0:T(8,128)S(1)} %bitcast.89, s32[2048]{0:T(1024)S(1)} %fusion.60), kind=kOutput, calls=%fused_computation.3 | convolution fusion | flops 3234332672 | bytes 25701376 | tf_op jit(solution)/shard_map/dot_general | solution.py:68
  183.3 1.6 fusion.4
  185.0 23.8 %all-reduce.8.cloned.1.call-done = f32[128,128]{0,1:T(8,128)} async-done(((f32[128,128]{0,1:T(8,128)}), f32[128,128]{0,1:T(8,128)}) %all-reduce.8.cloned.1.call-update) | async-done | bytes 65552 | tf_op jit(solution)/shard_map/psum | solution.py:54
  208.8 0.9 copy.16
  209.7 0.9 fusion.29
  210.5 11.7 %cholesky.44 = f32[128,128]{1,0:T(8,128)S(1)} custom-call(f32[128,128]{1,0:T(8,128)S(1)} %fusion.29), custom_call_target="Cholesky" | custom-call | tf_op jit(solution)/shard_map/jit(cholesky)/cholesky | solution.py:55
  222.3 0.7 compare_reduce_fusion.1
  223.0 0.7 fusion.12
  223.7 9.8 %custom-call.13 = f32[1,128,128]{1,2,0:T(8,128)S(1)} custom-call(f32[1,128,128]{2,1,0:T(8,128)S(1)} %fusion.12), custom_call_target="InvertDiagBlocksLowerTriangular" | custom-call | tf_op jit(solution)/shard_map/triangular_solve | solution.py:11
  233.5 0.6 convolution_subtract_fusion.2
  234.1 10.1 %fusion.77 = f32[2048,128]{1,0:T(8,128)} fusion(f32[2048,1024]{1,0:T(8,128)} %fusion.1, f32[1024,128]{1,0:T(8,128)S(1)} %convolution_subtract_fusion.2), kind=kOutput, calls=%fused_computation.122 | convolution fusion | flops 3221225472 | bytes 9961472 | tf_op jit(solution)/shard_map/dot_general | solution.py:76
  244.2 0.0 all-reduce.10.cloned.1.call-update
  244.2 0.0 all-reduce.12.cloned.1.call-start
  244.2 1.0 convolution_subtract_fusion.1
  245.2 16.6 %fusion.74 = f32[1024,128]{1,0:T(8,128)} fusion(f32[2048,1024]{1,0:T(8,128)} %fusion.1, f32[2048,128]{1,0:T(8,128)S(1)} %convolution_subtract_fusion.1), kind=kOutput, calls=%fused_computation.119 | convolution fusion | flops 3221225472 | bytes 9961472 | tf_op jit(solution)/shard_map/dot_general | solution.py:78
  261.8 41.8 %all-reduce.10.cloned.1.call-done = f32[2048,128]{1,0:T(8,128)} async-done(((f32[2048,128]{1,0:T(8,128)}), f32[2048,128]{1,0:T(8,128)}) %all-reduce.10.cloned.1.call-update) | async-done | bytes 1048592 | tf_op jit(solution)/shard_map/psum | solution.py:77
  303.7 3.7 fusion.79
  307.3 0.0 all-reduce.12.cloned.1.call-update
  307.3 46.2 %all-reduce.12.cloned.1.call-done = (f32[128,128]{1,0:T(8,128)}, f32[1024,128]{1,0:T(8,128)}, f32[128,128]{1,0:T(8,128)}) async-done(((f32[128,128]{1,0:T(8,128)}, f32[1024,128]{1,0:T(8,128)}, f32[128,128]{1,0:T(8,128)}), (f32[128,128]{1,0:T(8,128)}, f32[1024,128]{1,0:T(8,128)}, f32[128,128]{1,0:T(8,128)})) %all-reduce.12.cloned.1.call-update) | async-done | bytes 655376 | tf_op jit(solution)/shard_map/psum | solution.py:54
  353.6 1.1 fusion.25
  354.7 0.3 fusion.24
  355.0 0.1 copy.17
  355.1 11.7 %cholesky.55 = f32[128,128]{1,0:T(8,128)S(1)} custom-call(f32[128,128]{1,0:T(8,128)S(1)} %fusion.23), custom_call_target="Cholesky" | custom-call | tf_op jit(solution)/shard_map/jit(cholesky)/cholesky | solution.py:16
  366.8 0.6 compare_reduce_fusion
  367.4 0.6 fusion.13
  368.0 9.8 %custom-call.14 = f32[1,128,128]{1,2,0:T(8,128)S(1)} custom-call(f32[1,128,128]{2,1,0:T(8,128)S(1)} %fusion.13), custom_call_target="InvertDiagBlocksLowerTriangular" | custom-call | tf_op jit(solution)/shard_map/triangular_solve | solution.py:18
  377.8 0.3 fusion.19
  378.1 0.2 fusion.21
  378.3 1.0 fusion.80
  379.4 0.3 fusion.81
  379.7 1.8 fusion.75
  381.4 7.2 %fusion.76 = f32[2048,1024]{1,0:T(8,128)S(1)} fusion(f32[2048,128]{1,0:T(8,128)S(1)} %convolution_subtract_fusion.1, f32[128,1024]{1,0:T(8,128)S(1)} %fusion.75), kind=kOutput, calls=%fused_computation.121 | convolution fusion | flops 3221225472 | bytes 9961472 | tf_op jit(solution)/shard_map/dot_general | solution.py:82
  388.7 1.0 fusion.78
  389.7 1.0 convolution_subtract_fusion
  390.7 8.0 %subtract_bitcast_fusion = f32[1,2048,1,1024]{3,1,2,0:T(8,128)S(1)} fusion(f32[2048,1024]{1,0:T(8,128)S(1)} %bitcast.83, f32[2048,1024]{1,0:T(8,128)S(1)} %fusion.76, f32[2048,128]{1,0:T(8,128)S(1)} %convolution_subtract_fusion, f32[1024,128]{1,0:T(8,128)S(1)} %convolution_subtract_fusion.2), kind=kOutput, calls=%fused_computation.4 | convolution fusion | flops 3225419776 | bytes 26738688 | tf_op jit(solution)/shard_map/dot_general | solution.py:83
  398.7 16.1 %copy.18 = f32[1,2048,1,1024]{3,2,1,0:T(1,128)} copy(f32[1,2048,1,1024]{3,1,2,0:T(8,128)S(1)} %subtract_bitcast_fusion) | data formatting | bytes 16777216 | tf_op jit(solution)/shard_map/broadcast_in_dim | solution.py:88
  (18 shorter events, 0.2 us)
Async XLA Ops:
  6.5 151.3 %all-reduce.6.cloned.1.call-start = ((), (), s32[]{:S(2)}) async-start(), calls=%async_computation | async-start | bytes 8388608 | tf_op jit(solution)/shard_map/psum | solution.py:41
  12.3 196.4 %all-reduce.8.cloned.1.call-start = ((), (), s32[]{:S(2)}) async-start(), calls=%async_computation.1 | async-start | bytes 131072 | tf_op jit(solution)/shard_map/psum | solution.py:54
  167.5 136.2 %all-reduce.10.cloned.1.call-start = ((), (), s32[]{:S(2)}) async-start(), calls=%async_computation.2 | async-start | bytes 2097152 | tf_op jit(solution)/shard_map/psum | solution.py:77
  244.2 109.4 %all-reduce.12.cloned.1.call-start = ((), (), s32[]{:S(2)}) async-start(), calls=%async_computation.3 | async-start | bytes 1310720 | tf_op jit(solution)/shard_map/psum | solution.py:54
  379.6 9.0 %copy-start = (f32[2048,128]{1,0:T(8,128)S(1)}, f32[2048,128]{1,0:T(8,128)}, u32[]{:S(2)}) copy-start(f32[2048,128]{1,0:T(8,128)} %all-reduce.10.cloned.1.call-done) | copy-start | bytes 3145732
  379.6 11.0 %slice-start = ((s8[8388608]{0:T(1024)(128)(4,1)}), s8[4194304]{0:T(1024)(128)(4,1)S(1)}, s32[]{:S(2)}) async-start(s8[8388608]{0:T(1024)(128)(4,1)} %bitcast.82), calls=%async_computation.4 | async-start | bytes 8388608
  381.4 9.3 %slice-start.1 = ((s8[8388608]{0:T(1024)(128)(4,1)}), s8[4194304]{0:T(1024)(128)(4,1)S(1)}, s32[]{:S(2)}) async-start(s8[8388608]{0:T(1024)(128)(4,1)} %bitcast.82), calls=%async_computation.5 | async-start | bytes 8388608
Sparse Core Ops, SparseCore 0:
  12.9 144.9 all-reduce.5
  167.6 41.1 all-reduce.7
  244.3 59.2 all-reduce.9
  307.5 46.0 all-reduce.11
where the time goes:
time: 428 us; the launch traced here: 422 us
  waiting for transfers between devices  257 us (60%)
  matrix products  77.7 us (18%)
  other arithmetic  49.6 us (12%)
  local copies, waits for them, and re-layouts  22.7 us (5%)
  between operations  14.3 us (3%)
    psum x1, waiting for transfers between devices, per_device(): whole = lax.psum(partial_value, ('row', 'col'))  145 us
    psum x2, waiting for transfers between devices, per_device(): gram, top_rows = lax.psum((gram_part, top_part), 'row')  70 us
    psum x1, waiting for transfers between devices, per_device(): zrows = lax.psum(zpart, 'col')  41.8 us
    dot_general x1, matrix products, per_device(): lax.dot_general(refreshed, reflect_r, (((0,), (0,)), ((), ())), precision...  16.6 us
    broadcast_in_dim x1, local copies, waits for them, and re-layouts, per_device(): return (refreshed - first - second)[None, :, None, :]  16.1 us
    another operation x3, other arithmetic, per_device(): factor = jnp.linalg.cholesky(gram)  12.5 us
    another operation x3, other arithmetic, invert_shifted(): factor = jnp.linalg.cholesky(normal)  12.4 us
    dot_general x1, matrix products, per_device(): lax.dot_general(row_select, scols, (((0,), (1,)), ((), ())), precision=HIGH)  11 us
  transfers between devices with their start and end apart: 4, of which 4 were waited for; matrix products, arithmetic and copies ran while one was open for 8% of the time, Pallas kernels for 0%

commit v1 on v0

--- a/solution.py
+++ b/solution.py
@@ -38,7 +38,7 @@
     partial_value = lax.dot_general(
         psi, hcols, (((0,), (0,)), ((), ())), preferred_element_type=jnp.float32
     )
-    whole = lax.psum(partial_value, ("row", "col"))
+    whole = lax.psum(lax.psum(partial_value, "col"), "row")
     prow = lax.dynamic_index_in_dim(
         whole.reshape(tiles_r, n_row, TILE, panel), prow_id, 1, keepdims=False
     ).reshape(local_rows, panel)

time: 428 us -> 489 us (1.14)
  waiting for transfers between devices: 257 us -> 319 us
    psum x1 -> x2, waiting for transfers between devices: 145 us -> 206 us  [per_device(): whole = lax.psum(lax.psum(partial_value, 'col'), 'row')]
  transfers between devices with their start and end apart: 4 -> 5, of which waited for: 4 -> 5; matrix products, arithmetic and copies ran while one was open for 8% -> 7% of each run, Pallas kernels for 0% -> 0%
where the time goes in v1:
time: 489 us; the launch traced here: 483 us
  waiting for transfers between devices  319 us (65%)
  matrix products  77.7 us (16%)
  other arithmetic  49.6 us (10%)
  local copies, waits for them, and re-layouts  22.7 us (5%)
  between operations  14.3 us (3%)
    psum x2, waiting for transfers between devices, per_device(): whole = lax.psum(lax.psum(partial_value, 'col'), 'row')  206 us
    psum x2, waiting for transfers between devices, per_device(): gram, top_rows = lax.psum((gram_part, top_part), 'row')  70.7 us
    psum x1, waiting for transfers between devices, per_device(): zrows = lax.psum(zpart, 'col')  41.8 us
    dot_general x1, matrix products, per_device(): lax.dot_general(refreshed, reflect_r, (((0,), (0,)), ((), ())), precision...  16.6 us
    broadcast_in_dim x1, local copies, waits for them, and re-layouts, per_device(): return (refreshed - first - second)[None, :, None, :]  16.1 us
    another operation x3, other arithmetic, per_device(): factor = jnp.linalg.cholesky(gram)  12.5 us
    another operation x3, other arithmetic, invert_shifted(): factor = jnp.linalg.cholesky(normal)  12.4 us
    dot_general x1, matrix products, per_device(): lax.dot_general(row_select, scols, (((0,), (1,)), ((), ())), precision=HIGH)  11 us
  transfers between devices with their start and end apart: 5, of which 5 were waited for; matrix products, arithmetic and copies ran while one was open for 7% of the time, Pallas kernels for 0%

profile of v1, /device:TPU:0, one launch (start us, length us, event | category | flops | bytes accessed | tf_op | source)
XLA Modules:
  0.0 483.0 jit_solution(4359291769788836729)
XLA Ops:
  7.2 5.1 %convolution_bitcast_fusion = f32[8192,128]{0,1:T(8,128)} fusion(bf16[256,8192]{1,0:T(8,128)(2,1)} %param.7, bf16[256,128]{1,0:T(8,128)(2,1)} %param.8, pred[256]{0:T(512)(128)(4,1)S(1)} %iota_compare_fusion.9), kind=kOutput, calls=%fused_computation | convolution fusion | flops 536903680 | bytes 8454400 | tf_op jit(solution)/shard_map/dot_general | solution.py:38
  12.3 0.0 all-reduce.7.cloned.1.call-update
  12.3 0.0 all-reduce.9.cloned.1.call-start
  12.4 99.3 %all-reduce.7.cloned.1.call-done = f32[8192,128]{0,1:T(8,128)} async-done(((f32[8192,128]{0,1:T(8,128)}), f32[8192,128]{0,1:T(8,128)}) %all-reduce.7.cloned.1.call-update) | async-done | bytes 4194320 | tf_op jit(solution)/shard_map/psum | solution.py:41
  111.7 0.0 all-reduce.9.cloned.1.call-update
  111.7 0.0 all-reduce.11.cloned.1.call-start
  111.8 0.1 fusion.18
  111.9 106.7 %all-reduce.9.cloned.1.call-done = f32[8192,128]{0,1:T(8,128)} async-done(((f32[8192,128]{0,1:T(8,128)}), f32[8192,128]{0,1:T(8,128)}) %all-reduce.9.cloned.1.call-update) | async-done | bytes 4194320 | tf_op jit(solution)/shard_map/psum | solution.py:41
  218.6 5.6 %copy.11 = f32[8192,128]{1,0:T(8,128)} copy(f32[8192,128]{0,1:T(8,128)} %all-reduce.9.cloned.1.call-done) | data formatting | bytes 8388608 | tf_op jit(solution)/shard_map/psum | solution.py:41
  224.2 1.6 broadcast_select_fusion
  225.8 2.4 convolution_bitcast_fusion.1
  228.2 0.0 all-reduce.13.cloned.1.call-start
  228.3 3.6 fusion.10
  231.9 1.3 broadcast_select_fusion.1
  233.1 11.0 %fusion.1 = f32[2048,1024]{1,0:T(8,128)} fusion(f32[2048,1024]{1,0:T(8,128)S(1)} %fusion.10, f32[1,2048,1,1024]{3,2,1,0:T(1,128)} %param.10, pred[1024]{0:T(1024)(128)(4,1)S(1)} %broadcast_compare_fusion.1, pred[2048]{0:T(1024)(128)(4,1)S(1)} %broadcast_compare_fusion, f32[1024,128]{1,0:T(8,128)S(1)} %bitcast.89, s32[2048]{0:T(1024)S(1)} %fusion.60), kind=kOutput, calls=%fused_computation.3 | convolution fusion | flops 3234332672 | bytes 25701376 | tf_op jit(solution)/shard_map/dot_general | solution.py:68
  244.1 1.6 fusion.4
  245.8 24.5 %all-reduce.11.cloned.1.call-done = f32[128,128]{0,1:T(8,128)} async-done(((f32[128,128]{0,1:T(8,128)}), f32[128,128]{0,1:T(8,128)}) %all-reduce.11.cloned.1.call-update) | async-done | bytes 65552 | tf_op jit(solution)/shard_map/psum | solution.py:54
  270.2 0.9 copy.16
  271.2 0.9 fusion.29
  272.0 11.7 %cholesky.44 = f32[128,128]{1,0:T(8,128)S(1)} custom-call(f32[128,128]{1,0:T(8,128)S(1)} %fusion.29), custom_call_target="Cholesky" | custom-call | tf_op jit(solution)/shard_map/jit(cholesky)/cholesky | solution.py:55
  283.8 0.7 compare_reduce_fusion.1
  284.5 0.7 fusion.12
  285.2 9.8 %custom-call.13 = f32[1,128,128]{1,2,0:T(8,128)S(1)} custom-call(f32[1,128,128]{2,1,0:T(8,128)S(1)} %fusion.12), custom_call_target="InvertDiagBlocksLowerTriangular" | custom-call | tf_op jit(solution)/shard_map/triangular_solve | solution.py:11
  295.0 0.6 convolution_subtract_fusion.2
  295.6 10.1 %fusion.77 = f32[2048,128]{1,0:T(8,128)} fusion(f32[2048,1024]{1,0:T(8,128)} %fusion.1, f32[1024,128]{1,0:T(8,128)S(1)} %convolution_subtract_fusion.2), kind=kOutput, calls=%fused_computation.122 | convolution fusion | flops 3221225472 | bytes 9961472 | tf_op jit(solution)/shard_map/dot_general | solution.py:76
  305.7 0.0 all-reduce.15.cloned.1.call-start
  305.7 1.0 convolution_subtract_fusion.1
  306.7 16.6 %fusion.74 = f32[1024,128]{1,0:T(8,128)} fusion(f32[2048,1024]{1,0:T(8,128)} %fusion.1, f32[2048,128]{1,0:T(8,128)S(1)} %convolution_subtract_fusion.1), kind=kOutput, calls=%fused_computation.119 | convolution fusion | flops 3221225472 | bytes 9961472 | tf_op jit(solution)/shard_map/dot_general | solution.py:78
  323.3 41.8 %all-reduce.13.cloned.1.call-done = f32[2048,128]{1,0:T(8,128)} async-done(((f32[2048,128]{1,0:T(8,128)}), f32[2048,128]{1,0:T(8,128)}) %all-reduce.13.cloned.1.call-update) | async-done | bytes 1048592 | tf_op jit(solution)/shard_map/psum | solution.py:77
  365.1 3.7 fusion.79
  368.8 46.2 %all-reduce.15.cloned.1.call-done = (f32[128,128]{1,0:T(8,128)}, f32[1024,128]{1,0:T(8,128)}, f32[128,128]{1,0:T(8,128)}) async-done(((f32[128,128]{1,0:T(8,128)}, f32[1024,128]{1,0:T(8,128)}, f32[128,128]{1,0:T(8,128)}), (f32[128,128]{1,0:T(8,128)}, f32[1024,128]{1,0:T(8,128)}, f32[128,128]{1,0:T(8,128)})) %all-reduce.15.cloned.1.call-update) | async-done | bytes 655376 | tf_op jit(solution)/shard_map/psum | solution.py:54
  415.1 1.1 fusion.25
  416.2 0.3 fusion.24
  416.4 0.1 copy.17
  416.6 11.7 %cholesky.55 = f32[128,128]{1,0:T(8,128)S(1)} custom-call(f32[128,128]{1,0:T(8,128)S(1)} %fusion.23), custom_call_target="Cholesky" | custom-call | tf_op jit(solution)/shard_map/jit(cholesky)/cholesky | solution.py:16
  428.3 0.6 compare_reduce_fusion
  428.9 0.6 fusion.13
  429.5 9.8 %custom-call.14 = f32[1,128,128]{1,2,0:T(8,128)S(1)} custom-call(f32[1,128,128]{2,1,0:T(8,128)S(1)} %fusion.13), custom_call_target="InvertDiagBlocksLowerTriangular" | custom-call | tf_op jit(solution)/shard_map/triangular_solve | solution.py:18
  439.3 0.3 fusion.19
  439.6 0.2 fusion.21
  439.8 1.0 fusion.80
  440.9 0.3 fusion.81
  441.1 1.8 fusion.75
  442.9 7.2 %fusion.76 = f32[2048,1024]{1,0:T(8,128)S(1)} fusion(f32[2048,128]{1,0:T(8,128)S(1)} %convolution_subtract_fusion.1, f32[128,1024]{1,0:T(8,128)S(1)} %fusion.75), kind=kOutput, calls=%fused_computation.121 | convolution fusion | flops 3221225472 | bytes 9961472 | tf_op jit(solution)/shard_map/dot_general | solution.py:82
  450.2 1.0 fusion.78
  451.2 1.0 convolution_subtract_fusion
  452.2 8.0 %subtract_bitcast_fusion = f32[1,2048,1,1024]{3,1,2,0:T(8,128)S(1)} fusion(f32[2048,1024]{1,0:T(8,128)S(1)} %bitcast.83, f32[2048,1024]{1,0:T(8,128)S(1)} %fusion.76, f32[2048,128]{1,0:T(8,128)S(1)} %convolution_subtract_fusion, f32[1024,128]{1,0:T(8,128)S(1)} %convolution_subtract_fusion.2), kind=kOutput, calls=%fused_computation.4 | convolution fusion | flops 3225419776 | bytes 26738688 | tf_op jit(solution)/shard_map/dot_general | solution.py:83
  460.2 16.1 %copy.18 = f32[1,2048,1,1024]{3,2,1,0:T(1,128)} copy(f32[1,2048,1,1024]{3,1,2,0:T(8,128)S(1)} %subtract_bitcast_fusion) | data formatting | bytes 16777216 | tf_op jit(solution)/shard_map/broadcast_in_dim | solution.py:88
  (21 shorter events, 0.2 us)
Async XLA Ops:
  6.5 105.1 %all-reduce.7.cloned.1.call-start = ((), (), s32[]{:S(2)}) async-start(), calls=%async_computation | async-start | bytes 8388608 | tf_op jit(solution)/shard_map/psum | solution.py:41
  12.3 206.3 %all-reduce.9.cloned.1.call-start = ((), (), s32[]{:S(2)}) async-start(), calls=%async_computation.1 | async-start | bytes 8388608 | tf_op jit(solution)/shard_map/psum | solution.py:41
  111.7 158.6 %all-reduce.11.cloned.1.call-start = ((), (), s32[]{:S(2)}) async-start(), calls=%async_computation.2 | async-start | bytes 131072 | tf_op jit(solution)/shard_map/psum | solution.py:54
  228.2 136.9 %all-reduce.13.cloned.1.call-start = ((), (), s32[]{:S(2)}) async-start(), calls=%async_computation.3 | async-start | bytes 2097152 | tf_op jit(solution)/shard_map/psum | solution.py:77
  305.7 109.4 %all-reduce.15.cloned.1.call-start = ((), (), s32[]{:S(2)}) async-start(), calls=%async_computation.4 | async-start | bytes 1310720 | tf_op jit(solution)/shard_map/psum | solution.py:54
  441.1 9.0 %copy-start = (f32[2048,128]{1,0:T(8,128)S(1)}, f32[2048,128]{1,0:T(8,128)}, u32[]{:S(2)}) copy-start(f32[2048,128]{1,0:T(8,128)} %all-reduce.13.cloned.1.call-done) | copy-start | bytes 3145732
  441.1 11.0 %slice-start = ((s8[8388608]{0:T(1024)(128)(4,1)}), s8[4194304]{0:T(1024)(128)(4,1)S(1)}, s32[]{:S(2)}) async-start(s8[8388608]{0:T(1024)(128)(4,1)} %bitcast.82), calls=%async_computation.5 | async-start | bytes 8388608
  442.9 9.3 %slice-start.1 = ((s8[8388608]{0:T(1024)(128)(4,1)}), s8[4194304]{0:T(1024)(128)(4,1)S(1)}, s32[]{:S(2)}) async-start(s8[8388608]{0:T(1024)(128)(4,1)} %bitcast.82), calls=%async_computation.6 | async-start | bytes 8388608
Sparse Core Ops, SparseCore 0:
  12.4 99.1 all-reduce.6
  114.9 103.6 all-reduce.8
  228.4 41.8 all-reduce.10
  305.8 59.2 all-reduce.12
  368.9 46.0 all-reduce.14
